TPU v7x, 32 devices: a whole 2x2x4 slice. The times are simulated.
32 devices in a mesh: fsdp: 4 (over y, x), rep: 8 (over z, core).
Axes of the slice: x: 2, y: 2, z: 4, core: 2. Of those that a mesh axis runs over, the one named last changes fastest.
Arguments:
- hidden_in: bfloat16 [8192, 2048], P(('fsdp', 'rep'))
- out_grad: bfloat16 [8192, 2048], P(('fsdp', 'rep')), may hold values from -6 to 6
- attn_saved: bfloat16 [8192, 256], P(('fsdp', 'rep')), may hold values from -6 to 6
- row_lse: float32 [8192, 2], P(('fsdp', 'rep')), may hold values from 2.5 to 6
- w_qkv: bfloat16 [2048, 512], P('fsdp'), may hold values from -0.125 to 0.125
- w_out_t: bfloat16 [2048, 256], P('fsdp'), may hold values from -0.125 to 0.125
- doc_lengths: int32 [32, 4], P(('fsdp', 'rep')), may hold values from 1 to 128, 256 in all within a row
- seq_start: int32 [32], P(('fsdp', 'rep')), may hold values from 0 to 2047
Outputs:
- input_grad: bfloat16 [8192, 2048], P(('fsdp', 'rep'))
- grad_update: float32 [2048, 768], P('fsdp')
- grad_norm: float32 [], replicated
Inputs may be any that keep to these rules, and one draw needn't show every extreme that they name: `doc_lengths`: each row sums to 256; the longest document of each device has exactly 128 tokens.
All inputs are finite; a program needn't handle non-finite values.
Results may differ from a plain program's by a relative error of at most 0.014.
Values may be sent and summed in bfloat16 or wider, within the bound.
A program may use at most 64 MiB of HBM per device.

v0:
```python
import jax
import jax.numpy as jnp
from jax import lax
from jax.sharding import PartitionSpec as P

D = 2048
HEAD = 128


def rotary(values_in, positions, turn, head_size):
    rows = values_in.shape[0]
    heads_count = values_in.shape[1] // head_size
    half_size = head_size // 2
    inverse = 1000000.0 ** (-(jnp.arange(half_size, dtype=jnp.float32) * 2.0) / head_size)
    angles = positions.astype(jnp.float32)[:, None] * inverse[None, :]
    cosine = jnp.cos(angles)[:, None, :]
    sines = jnp.sin(angles)[:, None, :]
    shaped = values_in.reshape(rows, heads_count, head_size)
    first_half = shaped[:, :, :half_size]
    second_half = shaped[:, :, half_size:]
    result = jnp.concatenate(
        [
            first_half * cosine - turn * second_half * sines,
            second_half * cosine + turn * first_half * sines,
        ],
        axis=2,
    )
    return result.reshape(rows, heads_count * head_size)


def contract_rows(left, right):
    return lax.dot_general(
        left, right, (((0,), (0,)), ((), ())), preferred_element_type=jnp.float32
    )


def contract_cols(left, right):
    return lax.dot_general(
        left, right, (((1,), (1,)), ((), ())), preferred_element_type=jnp.float32
    )


def body(hidden_in, out_grad, attn_saved, row_lse, w_qkv, w_out_t, doc_lengths, seq_start):
    seq_rows = hidden_in.shape[0]
    head_size = HEAD
    query_width = attn_saved.shape[1]
    heads_count = row_lse.shape[1]
    scale = 1.0 / head_size**0.5
    tokens_part = hidden_in
    grads_part = out_grad
    proj = jnp.dot(
        tokens_part,
        lax.all_gather(w_qkv, "fsdp", axis=0, tiled=True),
        preferred_element_type=jnp.float32,
    )
    attn_full = jnp.dot(
        grads_part,
        lax.all_gather(w_out_t, "fsdp", axis=0, tiled=True),
        preferred_element_type=jnp.float32,
    )
    attn_grad = attn_full.astype(jnp.bfloat16)
    positions = seq_start[0] + jnp.arange(seq_rows, dtype=jnp.int32)
    queries = rotary(proj[:, :query_width], positions, 1.0, head_size).astype(jnp.bfloat16)
    keys = rotary(proj[:, query_width : query_width + head_size], positions, 1.0, head_size).astype(
        jnp.bfloat16
    )
    values_all = proj[:, query_width + head_size :].astype(jnp.bfloat16)
    ends = jnp.cumsum(doc_lengths[0])
    local_rows = jnp.arange(seq_rows, dtype=jnp.int32)
    documents = jnp.sum((local_rows[:, None] >= ends[None, :]).astype(jnp.int32), axis=1)
    block_rows = min(seq_rows, 512)
    block_count = seq_rows // block_rows

    def attend_block(carry, inputs):
        key_grad, value_grad = carry
        query_rows, grad_rows, saved_rows, lse_rows, index_rows, doc_rows = inputs
        allowed = (doc_rows[:, None] == documents[None, :]) & (
            local_rows[None, :] <= index_rows[:, None]
        )
        query_parts = []
        for head_index in range(heads_count):
            lower = head_index * head_size
            query_head = query_rows[:, lower : lower + head_size]
            scores = contract_cols(query_head, keys) * scale
            probs = jnp.where(
                allowed, jnp.exp(scores - lse_rows[:, head_index : head_index + 1]), 0.0
            )
            grad_head = grad_rows[:, lower : lower + head_size]
            dprobs = contract_cols(grad_head, values_all)
            delta = jnp.sum(
                grad_head.astype(jnp.float32)
                * saved_rows[:, lower : lower + head_size].astype(jnp.float32),
                axis=1,
                keepdims=True,
            )
            dscores = (probs * (dprobs - delta) * scale).astype(jnp.bfloat16)
            probs_low = probs.astype(jnp.bfloat16)
            value_grad = value_grad + contract_rows(probs_low, grad_head)
            query_parts.append(jnp.dot(dscores, keys, preferred_element_type=jnp.float32))
            key_grad = key_grad + contract_rows(dscores, query_head)
        return ((key_grad, value_grad), jnp.concatenate(query_parts, axis=1))

    block_inputs = (
        queries.reshape(block_count, block_rows, query_width),
        attn_grad.reshape(block_count, block_rows, query_width),
        attn_saved.reshape(block_count, block_rows, query_width),
        row_lse.reshape(block_count, block_rows, heads_count),
        local_rows.reshape(block_count, block_rows),
        documents.reshape(block_count, block_rows),
    )
    zero_grad = jnp.zeros((seq_rows, head_size), jnp.float32)
    (key_grad, value_grad), query_blocks = lax.scan(
        attend_block, (zero_grad, zero_grad), block_inputs
    )
    query_grad = rotary(
        query_blocks.reshape(seq_rows, query_width), positions, -1.0, head_size
    ).astype(jnp.bfloat16)
    key_grad = rotary(key_grad, positions, -1.0, head_size).astype(jnp.bfloat16)
    d_qkv = jnp.concatenate([query_grad, key_grad, value_grad.astype(jnp.bfloat16)], axis=1)
    input_full = contract_cols(d_qkv, lax.all_gather(w_qkv, "fsdp", axis=0, tiled=True))
    input_grad = input_full.astype(jnp.bfloat16)
    tokens_part = hidden_in
    grads_part = out_grad
    shard_sum = lax.psum_scatter(
        jnp.concatenate(
            [contract_rows(tokens_part, d_qkv), contract_rows(grads_part, attn_saved)], axis=1
        ).astype(jnp.bfloat16),
        "fsdp",
        scatter_dimension=0,
        tiled=True,
    ).astype(jnp.float32)
    grads = lax.psum(shard_sum, "rep")
    norm_sq = lax.psum(jnp.sum(grads * grads), "fsdp")
    grad_update = grads * lax.rsqrt(norm_sq / (D * grads.shape[1]) + 1e-06)
    return (input_grad, grad_update, jnp.sqrt(norm_sq))


def solution(mesh):
    in_specs = (
        P(("fsdp", "rep"), None),
        P(("fsdp", "rep"), None),
        P(("fsdp", "rep"), None),
        P(("fsdp", "rep"), None),
        P("fsdp", None),
        P("fsdp", None),
        P(("fsdp", "rep"), None),
        P(("fsdp", "rep")),
    )
    out_specs = (P(("fsdp", "rep"), None), P("fsdp", None), P())
    return jax.shard_map(body, mesh=mesh, in_specs=in_specs, out_specs=out_specs, check_vma=False)
```

profile of v0, /device:TPU:0, one launch (start us, length us, event | category | flops | bytes accessed | tf_op | source)
XLA Modules:
  0.0 219.8 jit_solution(17886597577698370556)
XLA Ops:
  9.4 0.9 fusion.49
  10.3 0.7 copy.36
  11.0 0.7 copy.37
  11.7 0.8 reduce-window.8
  13.2 1.3 fusion.50
  14.6 1.2 broadcast_multiply_fusion.1
  15.8 1.4 convolution_convert_fusion.2
  17.2 21.9 %all-gather.5.cloned.1.call-done = bf16[2048,256]{1,0:T(8,128)(2,1)} async-done(((bf16[512,256]{1,0:T(8,128)(2,1)}), bf16[2048,256]{1,0:T(8,128)(2,1)}) %all-gather.5.cloned.1.call-update) | async-done | bytes 1048592 | tf_op jit(solution)/shard_map/all_gather | solution.py:58
  39.1 1.7 convolution_convert_fusion.3
  40.8 0.9 multiply_reduce_fusion.1
  41.8 34.4 %all-gather.3.cloned.1.call-done = bf16[2048,512]{1,0:T(8,128)(2,1)} async-done(((bf16[512,512]{1,0:T(8,128)(2,1)}), bf16[2048,512]{1,0:T(8,128)(2,1)}) %all-gather.3.cloned.1.call-update) | async-done | bytes 2097168 | tf_op jit(solution)/shard_map/all_gather | solution.py:53
  76.1 2.3 %fusion.51 = f32[256,512]{1,0:T(8,128)S(1)} fusion(bf16[256,2048]{1,0:T(8,128)(2,1)S(1)} %copy-done, bf16[2048,512]{1,0:T(8,128)(2,1)} %all-gather.3.cloned.1.call-done), kind=kOutput, calls=%fused_computation.89 | convolution fusion | flops 536870912 | bytes 3670016 | tf_op jit(solution)/shard_map/dot_general | solution.py:51
  78.6 1.0 fusion.28
  80.6 1.0 fusion.10
  84.4 1.2 subtract_convert_fusion
  86.0 0.7 fusion
  86.7 1.9 pad_maximum_fusion
  88.7 44.1 %reduce-scatter.2.cloned.1.call-done = bf16[512,768]{0,1:T(8,128)(2,1)} async-done(((bf16[2048,768]{0,1:T(8,128)(2,1)}), bf16[512,768]{0,1:T(8,128)(2,1)}) %reduce-scatter.2.cloned.1.call-update) | async-done | bytes 786448 | tf_op jit(solution)/shard_map/reduce_scatter | solution.py:124
  132.7 59.9 %all-reduce.1 = f32[512,768]{0,1:T(8,128)S(1)} all-reduce(bf16[512,768]{0,1:T(8,128)(2,1)} %reduce-scatter.2.cloned.1.call-done), channel_id=1, replica_groups=mesh['fsdp'=4,'rep'=8] {'rep'}, use_global_device_ids=true, to_apply=%region_5.6 | all-reduce | flops 393216 | bytes 2359296 | tf_op jit(solution)/shard_map/psum | solution.py:132
  192.6 1.0 multiply_reduce_fusion
  193.6 3.3 %convolution_convert_fusion.1 = bf16[256,2048]{1,0:T(8,128)(2,1)} fusion(bf16[2048,512]{1,0:T(8,128)(2,1)} %all-gather.3.cloned.1.call-done, bf16[256,128]{1,0:T(8,128)(2,1)S(1)} %copy.33, bf16[256,128]{1,0:T(8,128)(2,1)S(1)} %copy.32, bf16[256,256]{1,0:T(8,128)(2,1)S(1)} %bitcast.49), kind=kOutput, calls=%fused_computation.3 | convolution fusion | flops 538181632 | bytes 3407872 | tf_op jit(solution)/shard_map/dot_general | solution.py:38
  196.9 9.5 %psum.15 = f32[]{:T(128)} all-reduce(f32[]{:T(128)} %multiply_reduce_fusion), channel_id=1, replica_groups=mesh['fsdp'=4,'rep'=8] {'fsdp'}, use_global_device_ids=true, to_apply=%region_7.8 | all-reduce | flops 1 | bytes 8 | tf_op jit(solution)/shard_map/psum | solution.py:133
  207.8 1.3 broadcast_multiply_fusion
  209.1 3.0 %copy.34 = f32[512,768]{1,0:T(8,128)} copy(f32[512,768]{0,1:T(8,128)} %broadcast_multiply_fusion) | data formatting | bytes 3145728
  (47 shorter events, 6.4 us)
Async XLA Ops:
  7.2 69.0 %copy-start = (bf16[256,2048]{1,0:T(8,128)(2,1)S(1)}, bf16[256,2048]{1,0:T(8,128)(2,1)}, u32[]{:S(2)}) copy-start(bf16[256,2048]{1,0:T(8,128)(2,1)} %param.8) | copy-start | bytes 3145732
  7.2 8.6 %copy-start.1 = (bf16[256,2048]{1,0:T(8,128)(2,1)S(1)}, bf16[256,2048]{1,0:T(8,128)(2,1)}, u32[]{:S(2)}) copy-start(bf16[256,2048]{1,0:T(8,128)(2,1)} %param.9) | copy-start | bytes 3145732
  7.2 31.9 %all-gather.5.cloned.1.call-start = ((), (), s32[]{:S(2)}) async-start(), calls=%async_computation.2 | async-start | bytes 1310720 | tf_op jit(solution)/shard_map/all_gather | solution.py:58
  7.9 68.2 %all-gather.3.cloned.1.call-start = ((), (), s32[]{:S(2)}) async-start(), calls=%async_computation.1 | async-start | bytes 2621440 | tf_op jit(solution)/shard_map/all_gather | solution.py:53
  8.7 124.0 %reduce-scatter.2.cloned.1.call-start = ((), (), s32[]{:S(2)}) async-start(), calls=%async_computation.3 | async-start | bytes 3932160 | tf_op jit(solution)/shard_map/reduce_scatter | solution.py:124
  79.7 2.3 %copy-start.2 = (bf16[256,1,64]{0,2,1:T(8,128)(2,1)S(1)}, bf16[256,1,64]{0,2,1:T(8,128)(2,1)}, u32[]{:S(2)}) copy-start(bf16[256,1,64]{0,2,1:T(8,128)(2,1)} %get-tuple-element.64) | copy-start | bytes 98308
  79.7 2.3 %copy-start.3 = (bf16[256,1,64]{0,2,1:T(8,128)(2,1)S(1)}, bf16[256,1,64]{0,2,1:T(8,128)(2,1)}, u32[]{:S(2)}) copy-start(bf16[256,1,64]{0,2,1:T(8,128)(2,1)} %get-tuple-element.65) | copy-start | bytes 98308
  79.7 2.7 %copy-start.4 = (f32[256,1]{0,1:T(1,128)S(1)}, f32[256,1]{0,1:T(1,128)}, u32[]{:S(2)}) copy-start(f32[256,1]{0,1:T(1,128)} %get-tuple-element.68) | copy-start | bytes 3076
  79.7 2.7 %copy-start.5 = (s32[256]{0:T(256)S(1)}, s32[256]{0:T(256)}, u32[]{:S(2)}) copy-start(s32[256]{0:T(256)} %convert_reduce_fusion) | copy-start | bytes 3076
Sparse Core Ops, SparseCore 0:
  9.8 29.2 all-gather.4
  40.9 35.1 all-gather.2
  88.8 43.8 reduce-scatter.1
where the time goes:
time: 220 us
  waiting for transfers between devices  102 us (46%)
  blocking collectives  69.4 us (32%)
  between operations  17.2 us (8%)
  matrix products  12.2 us (6%)
  other arithmetic  11.5 us (5%)
  local copies, waits for them, and re-layouts  7.61 us (3%)
    psum x1, blocking collectives, body(): grads = lax.psum(shard_sum, 'rep')  59.9 us
    reduce_scatter x1, waiting for transfers between devices, body(): lax.psum_scatter(jnp.concatenate([contract_rows(tokens_part, d_qkv), cont...  44.1 us
    all_gather x1, waiting for transfers between devices, body(): lax.all_gather(w_qkv, 'fsdp', axis=0, tiled=True)  34.4 us
    all_gather x1, waiting for transfers between devices, body(): lax.all_gather(w_out_t, 'fsdp', axis=0, tiled=True)  21.9 us
    psum x1, blocking collectives, body(): norm_sq = lax.psum(jnp.sum(grads * grads), 'fsdp')  9.53 us
    unnamed x20, local copies, waits for them, and re-layouts  4.97 us
    dot_general x5, matrix products, contract_cols(): lax.dot_general(left, right, (((1,), (1,)), ((), ())), preferred_element_...  4.91 us
  transfers between devices with their start and end apart: 3, of which 3 were waited for; matrix products, arithmetic and copies ran while one was open for 5% of the time, Pallas kernels for 0%

commit v1 on v0

--- a/solution.py
+++ b/solution.py
@@ -129,7 +129,7 @@
         scatter_dimension=0,
         tiled=True,
     ).astype(jnp.float32)
-    grads = lax.psum(shard_sum, "rep")
+    grads = jnp.sum(lax.all_gather(shard_sum, "rep"), axis=0)
     norm_sq = lax.psum(jnp.sum(grads * grads), "fsdp")
     grad_update = grads * lax.rsqrt(norm_sq / (D * grads.shape[1]) + 1e-06)
     return (input_grad, grad_update, jnp.sqrt(norm_sq))

time: 220 us -> 311 us (1.41)
  waiting for transfers between devices: 102 us -> 218 us
  blocking collectives: 69.4 us -> 10.4 us
  local copies, waits for them, and re-layouts: 7.61 us -> 29.3 us
  other arithmetic: 11.5 us -> 21.5 us
    all_gather x0 -> x1, waiting for transfers between devices: none -> 117 us  [body(): grads = jnp.sum(lax.all_gather(shard_sum, 'rep'), axis=0)]
    psum x1 -> x0, blocking collectives: 59.9 us -> none  [body(): grads = lax.psum(shard_sum, 'rep')]
    unnamed x20 -> x23, local copies, waits for them, and re-layouts: 4.97 us -> 26.6 us
    reduce_sum x0 -> x1, other arithmetic: none -> 7.57 us  [body(): grads = jnp.sum(lax.all_gather(shard_sum, 'rep'), axis=0)]
  transfers between devices with their start and end apart: 3 -> 4, of which waited for: 3 -> 4; matrix products, arithmetic and copies ran while one was open for 5% -> 3% of each run, Pallas kernels for 0% -> 0%
where the time goes in v1:
time: 311 us; the launch traced here: 310 us
  waiting for transfers between devices  218 us (70%)
  local copies, waits for them, and re-layouts  29.3 us (9%)
  other arithmetic  21.5 us (7%)
  between operations  17.2 us (6%)
  matrix products  12.9 us (4%)
  blocking collectives  10.4 us (3%)
    all_gather x1, waiting for transfers between devices, body(): grads = jnp.sum(lax.all_gather(shard_sum, 'rep'), axis=0)  117 us
    reduce_scatter x1, waiting for transfers between devices, body(): lax.psum_scatter(jnp.concatenate([contract_rows(tokens_part, d_qkv), cont...  43.8 us
    all_gather x1, waiting for transfers between devices, body(): lax.all_gather(w_qkv, 'fsdp', axis=0, tiled=True)  34.4 us
    unnamed x23, local copies, waits for them, and re-layouts  26.6 us
    all_gather x1, waiting for transfers between devices, body(): lax.all_gather(w_out_t, 'fsdp', axis=0, tiled=True)  22 us
    psum x1, blocking collectives, body(): norm_sq = lax.psum(jnp.sum(grads * grads), 'fsdp')  10.4 us
    reduce_sum x1, other arithmetic, body(): grads = jnp.sum(lax.all_gather(shard_sum, 'rep'), axis=0)  7.57 us
  transfers between devices with their start and end apart: 4, of which 4 were waited for; matrix products, arithmetic and copies ran while one was open for 3% of the time, Pallas kernels for 0%

profile of v1, /device:TPU:0, one launch (start us, length us, event | category | flops | bytes accessed | tf_op | source)
XLA Modules:
  0.0 310.1 jit_solution(17135474807730895993)
XLA Ops:
  9.4 0.9 fusion.49
  13.2 1.3 fusion.50
  14.6 1.2 broadcast_multiply_fusion.1
  15.8 1.4 convolution_convert_fusion.2
  17.1 22.0 %all-gather.7.cloned.1.call-done = bf16[2048,256]{1,0:T(8,128)(2,1)} async-done(((bf16[512,256]{1,0:T(8,128)(2,1)}), bf16[2048,256]{1,0:T(8,128)(2,1)}) %all-gather.7.cloned.1.call-update) | async-done | bytes 1048592 | tf_op jit(solution)/shard_map/all_gather | solution.py:58
  39.1 1.7 convolution_convert_fusion.3
  40.8 0.9 multiply_reduce_fusion.1
  41.8 34.4 %all-gather.5.cloned.1.call-done = bf16[2048,512]{1,0:T(8,128)(2,1)} async-done(((bf16[512,512]{1,0:T(8,128)(2,1)}), bf16[2048,512]{1,0:T(8,128)(2,1)}) %all-gather.5.cloned.1.call-update) | async-done | bytes 2097168 | tf_op jit(solution)/shard_map/all_gather | solution.py:53
  76.1 2.3 fusion.51
  78.6 0.9 fusion.28
  80.6 1.0 fusion.10
  82.0 0.9 fusion.47
  84.7 0.9 pad_maximum_fusion.1
  87.4 1.9 pad_maximum_fusion
  89.5 43.8 %reduce-scatter.2.cloned.1.call-done = bf16[512,768]{0,1:T(8,128)(2,1)} async-done(((bf16[2048,768]{0,1:T(8,128)(2,1)}), bf16[512,768]{0,1:T(8,128)(2,1)}) %reduce-scatter.2.cloned.1.call-update) | async-done | bytes 786448 | tf_op jit(solution)/shard_map/reduce_scatter | solution.py:124
  133.4 2.5 all_gather.21
  135.9 116.9 %all-gather.9.cloned.1.call-done = f32[4096,768]{0,1:T(8,128)} async-done(((f32[512,768]{0,1:T(8,128)}), f32[4096,768]{0,1:T(8,128)}) %all-gather.9.cloned.1.call-update) | async-done | bytes 12582928 | tf_op jit(solution)/shard_map/all_gather | solution.py:132
  252.7 21.7 %copy.49 = f32[96,8,8,512]{3,2,1,0:T(8,128)} copy(f32[96,8,8,512]{3,1,2,0:T(8,128)} %bitcast.45) | data formatting | bytes 25165824
  274.4 7.6 %bitcast_reduce_fusion = f32[512,768]{0,1:T(8,128)S(1)} fusion(f32[96,8,8,512]{3,2,1,0:T(8,128)} %copy.49), kind=kLoop, calls=%fused_computation | loop fusion | flops 2752512 | bytes 14155776 | tf_op jit(solution)/shard_map/reduce_sum | solution.py:132
  282.0 1.0 multiply_reduce_fusion
  283.0 3.3 %convolution_convert_fusion.1 = bf16[256,2048]{1,0:T(8,128)(2,1)} fusion(bf16[2048,512]{1,0:T(8,128)(2,1)} %all-gather.5.cloned.1.call-done, bf16[256,128]{1,0:T(8,128)(2,1)S(1)} %copy.40, bf16[256,128]{1,0:T(8,128)(2,1)S(1)} %copy.39, bf16[256,256]{1,0:T(8,128)(2,1)S(1)} %bitcast.55), kind=kOutput, calls=%fused_computation.4 | convolution fusion | flops 538181632 | bytes 3407872 | tf_op jit(solution)/shard_map/dot_general | solution.py:38
  286.3 10.4 %psum.7 = f32[]{:T(128)} all-reduce(f32[]{:T(128)} %multiply_reduce_fusion), channel_id=1, replica_groups=mesh['fsdp'=4,'rep'=8] {'fsdp'}, use_global_device_ids=true, to_apply=%region_7.8 | all-reduce | flops 1 | bytes 8 | tf_op jit(solution)/shard_map/psum | solution.py:133
  298.1 1.3 broadcast_multiply_fusion
  299.4 3.0 copy.41
  (54 shorter events, 9.7 us)
Async XLA Ops:
  7.2 69.0 %copy-start = (bf16[256,2048]{1,0:T(8,128)(2,1)S(1)}, bf16[256,2048]{1,0:T(8,128)(2,1)}, u32[]{:S(2)}) copy-start(bf16[256,2048]{1,0:T(8,128)(2,1)} %param.8) | copy-start | bytes 3145732
  7.2 8.6 %copy-start.1 = (bf16[256,2048]{1,0:T(8,128)(2,1)S(1)}, bf16[256,2048]{1,0:T(8,128)(2,1)}, u32[]{:S(2)}) copy-start(bf16[256,2048]{1,0:T(8,128)(2,1)} %param.9) | copy-start | bytes 3145732
  7.2 31.9 %all-gather.7.cloned.1.call-start = ((), (), s32[]{:S(2)}) async-start(), calls=%async_computation.2 | async-start | bytes 1310720 | tf_op jit(solution)/shard_map/all_gather | solution.py:58
  7.9 68.2 %all-gather.5.cloned.1.call-start = ((), (), s32[]{:S(2)}) async-start(), calls=%async_computation.1 | async-start | bytes 2621440 | tf_op jit(solution)/shard_map/all_gather | solution.py:53
  8.7 124.7 %reduce-scatter.2.cloned.1.call-start = ((), (), s32[]{:S(2)}) async-start(), calls=%async_computation.3 | async-start | bytes 3932160 | tf_op jit(solution)/shard_map/reduce_scatter | solution.py:124
  79.7 2.3 copy-start.3
  79.7 2.3 copy-start.4
  79.7 3.4 %copy-start.5 = (f32[256,1]{0,1:T(1,128)S(1)}, f32[256,1]{0,1:T(1,128)}, u32[]{:S(2)}) copy-start(f32[256,1]{0,1:T(1,128)} %get-tuple-element.68) | copy-start | bytes 3076
  79.7 3.4 %copy-start.6 = (s32[256]{0:T(256)S(1)}, s32[256]{0:T(256)}, u32[]{:S(2)}) copy-start(s32[256]{0:T(256)} %convert_reduce_fusion) | copy-start | bytes 3076
  83.5 2.5 copy-start.2
  89.3 163.4 %all-gather.9.cloned.1.call-start = ((), (), s32[]{:S(2)}) async-start(), calls=%async_computation.4 | async-start | bytes 14155776 | tf_op jit(solution)/shard_map/all_gather | solution.py:132
Sparse Core Ops, SparseCore 0:
  9.8 29.2 all-gather.6
  40.9 35.1 all-gather.4
  89.4 43.8 reduce-scatter.1
  136.0 116.6 all-gather.8
